TPU v7x, 128 devices: a whole 4x4x4 slice. The times are simulated.
128 devices in a mesh: row: 2 (over core), col: 64 (over z, y, x).
Axes of the slice: x: 4, y: 4, z: 4, core: 2. Of those that a mesh axis runs over, the one named last changes fastest.
Arguments:
- w_one: float32 [2, 64, 2, 128, 512], P('row', 'col')
- w_two: float32 [2, 64, 2, 512, 128], P('row', 'col')
- inputs: bfloat16 [2, 64, 3, 2048, 128], P('row', 'col')
- targets: bfloat16 [2, 64, 3, 2048, 128], P('row', 'col')
Outputs:
- output 1: float32 [2, 64, 2, 128, 512], P('row', 'col')
- output 2: float32 [2, 64, 2, 512, 128], P('row', 'col')
All inputs are finite; a program needn't handle non-finite values.
Results may differ from a plain program's by a relative error of at most 0.00126359.
Values are sent between devices in bfloat16 or wider.
A program may use at most 1 GiB of HBM per device.

v0:
```python
import functools

import jax
import jax.numpy as jnp
from jax import lax
from jax.experimental import pallas as pl
from jax.experimental.pallas import tpu as pltpu
from jax.sharding import PartitionSpec as P

LEARN_RATE = 1.5
NORM_EPS = 1e-6
GELU_C = 0.7978845608028654
GELU_K = 0.044715
MESH = pl.DeviceIdType.MESH
F32 = jnp.float32
BF16 = jnp.bfloat16
N_DEST = 3
N_PART = 2


def dot(lhs, rhs):
    return lax.dot_general(lhs, rhs, (((1,), (0,)), ((), ())), preferred_element_type=F32)


def dot_rhs_t(lhs, rhs):
    return lax.dot_general(lhs, rhs, (((1,), (1,)), ((), ())), preferred_element_type=F32)


def gelu_and_slope(z):
    cubic = (GELU_C * GELU_K * z) * z
    th = jnp.tanh(z * (GELU_C + cubic))
    half = 0.5 + 0.5 * th
    act = z * half
    slope = half + act * (1.0 - th) * (GELU_C + 3.0 * cubic)
    return act, slope


def kernel(n_rows, n_cols, w1_hbm, w2_hbm, x_hbm, t_hbm, o1_hbm, o2_hbm,
           xs, ts, w2_in, master, wlo, act, slope, n_lo, n_tr, inv_b, hid, err, err_lo, err_tr, grad_a, grad_b,
           send, recv, in_sem, out_sem, send_sem, recv_sem):
    n_steps, batch, width = xs.shape
    hidden = act.shape[2]
    part = hidden // N_PART
    row, col = lax.axis_index("row"), lax.axis_index("col")
    nxt, prv = lax.rem(col + 1, n_cols), lax.rem(col + n_cols - 1, n_cols)
    dests = ((row, nxt), (row, prv), (lax.rem(row + 1, n_rows), col))

    def start(src, dst, idx):
        cp = pltpu.make_async_copy(src, dst, in_sem.at[idx])
        cp.start()
        return cp

    cp_x, cp_t = [None] * n_steps, [None] * n_steps
    cp_x[0] = start(x_hbm.at[0], xs.at[0], 0)
    cp_w1 = [start(w1_hbm.at[l], master.at[2 * l], 1 + l) for l in range(2)]
    cp_w2 = [start(w2_hbm.at[l], w2_in.at[l], 3 + l) for l in range(2)]
    for t in range(n_steps):
        if t:
            cp_x[t] = start(x_hbm.at[t], xs.at[t], 4 + 2 * t)
        cp_t[t] = start(t_hbm.at[t], ts.at[t], 5 + 2 * t)

    barrier = pltpu.get_barrier_semaphore()
    for dest in dests:
        pl.semaphore_signal(barrier, inc=1, device_id=dest, device_id_type=MESH)

    def over_rows(size, body, unroll=1):
        def step(i, carry):
            body(pl.ds(pl.multiple_of(i * size, size), size))
            return carry
        lax.fori_loop(0, batch // size, step, 0, unroll=unroll)

    def norm_of(x):
        return lax.rsqrt(jnp.mean(x * x, axis=-1, keepdims=True) + NORM_EPS)

    def prepare(t):
        def body(rows):
            x = xs[t, rows, :].astype(F32)
            n = (x * norm_of(x)).astype(BF16)
            n_lo[0, rows, :] = n
            n_tr[0, :, rows] = n.T
        over_rows(512, body)

    def hidden_phase(l, cols, sub=128):
        def body(rows):
            for s in range(rows.size // sub):
                r = pl.ds(rows.start + s * sub, sub)
                a, d = gelu_and_slope(dot(n_lo[l, r, :], wlo[2 * l, :, cols]))
                act[l, r, cols] = a.astype(BF16)
                slope[l, r, cols] = d
        over_rows(512, body)

    def out0_phase(t):
        def body(rows):
            o = dot_rhs_t(act[0, rows, :], wlo[1])
            h = (xs[t, rows, :].astype(F32) + o).astype(BF16)
            hid[rows, :] = h
            x = h.astype(F32)
            inv = norm_of(x)
            n = (x * inv).astype(BF16)
            inv_b[rows, :] = jnp.broadcast_to(inv, x.shape)
            n_lo[1, rows, :] = n
            n_tr[1, :, rows] = n.T
        over_rows(512, body)

    def out1_phase(t):
        loss_scale = 2.0 / (batch * width)

        def body(rows):
            o = dot_rhs_t(act[1, rows, :], wlo[3])
            h = (hid[rows, :].astype(F32) + o).astype(BF16)
            e = loss_scale * (h.astype(F32) - ts[t, rows, :].astype(F32))
            lo = e.astype(BF16)
            err[rows, :] = e
            err_lo[rows, :] = lo
            err_tr[:, rows] = lo.T
        over_rows(512, body)

    def update(t, u, grad):
        q = master[u] - LEARN_RATE * grad
        master[u] = q
        lo = q.astype(BF16)
        for h in range(N_PART):
            send[t, u * N_PART + h] = lo[:, h * part:(h + 1) * part]

    def copy_of(t, d, k):
        return pltpu.make_async_remote_copy(
            src_ref=send.at[t, k], dst_ref=recv.at[t, d, k], send_sem=send_sem.at[t, d, k],
            recv_sem=recv_sem.at[t, d, k], device_id=dests[d], device_id_type=MESH)

    def push(t, *ks):
        for k in ks:
            for d in range(N_DEST):
                copy_of(t, d, k).start()

    def combine(t, k):
        for d in range(N_DEST):
            copy_of(t, d, k).wait_recv()
        u, h = divmod(k, N_PART)
        cols = slice(h * part, (h + 1) * part)
        other = recv[t, 2, k].astype(F32)
        total = master[u, :, cols] + recv[t, 0, k].astype(F32) + recv[t, 1, k].astype(F32) + other + other
        p = total / 5.0
        master[u, :, cols] = p
        if t < n_steps - 1:
            wlo[u, :, cols] = p.astype(BF16)

    def back1_phase():
        grad_a[...] = jnp.zeros_like(grad_a)
        grad_b[...] = jnp.zeros_like(grad_b)

        def body(rows):
            d_act = dot(err_lo[rows, :], wlo[3])
            dz = (d_act * slope[1, rows, :]).astype(BF16)
            grad_a[...] += dot(n_tr[1, :, rows], dz)
            m = dot_rhs_t(dz, wlo[2])
            inv = inv_b[rows, :]
            n = hid[rows, :].astype(F32) * inv
            e = err[rows, :] + inv * (m - n * jnp.mean(m * n, axis=-1, keepdims=True))
            lo = e.astype(BF16)
            err_lo[rows, :] = lo
            grad_b[...] += dot(lo.T, act[0, rows, :])
        over_rows(512, body)

    def back0_phase():
        grad_a[...] = jnp.zeros_like(grad_a)

        def body(rows):
            d_act = dot(err_lo[rows, :], wlo[1])
            dz = (d_act * slope[0, rows, :]).astype(BF16)
            grad_a[...] += dot(n_tr[0, :, rows], dz)
        over_rows(512, body)

    halves = [slice(h * part, (h + 1) * part) for h in range(N_PART)]
    cp_x[0].wait()
    prepare(0)
    for l in range(2):
        cp_w1[l].wait()
        wlo[2 * l] = master[2 * l].astype(BF16)
    for l in range(2):
        cp_w2[l].wait()
        w = w2_in[l].T
        master[2 * l + 1] = w
        wlo[2 * l + 1] = w.astype(BF16)

    for t in range(n_steps):
        for h in range(N_PART):
            if t:
                combine(t - 1, h)
            hidden_phase(0, halves[h])
        if t:
            combine(t - 1, 2)
            combine(t - 1, 3)
        out0_phase(t)
        for h in range(N_PART):
            if t:
                combine(t - 1, 4 + h)
            hidden_phase(1, halves[h])
        cp_t[t].wait()
        if t:
            combine(t - 1, 6)
            combine(t - 1, 7)
        out1_phase(t)
        update(t, 3, dot(err_tr[...], act[1]))
        if t == 0:
            pl.semaphore_wait(barrier, N_DEST)
        push(t, 6, 7)
        back1_phase()
        update(t, 2, grad_a[...])
        update(t, 1, grad_b[...])
        back0_phase()
        update(t, 0, grad_a[...])
        push(t, 0, 1, 2, 3, 4, 5)
        if t < n_steps - 1:
            cp_x[t + 1].wait()
            prepare(t + 1)

    last = n_steps - 1
    outs = []
    for u in (3, 0, 1, 2):
        l = u // 2
        for h in range(N_PART):
            combine(last, u * N_PART + h)
        if u % 2:
            w2_in[l] = master[u].T
            cp = pltpu.make_async_copy(w2_in.at[l], o2_hbm.at[l], out_sem.at[u])
        else:
            cp = pltpu.make_async_copy(master.at[u], o1_hbm.at[l], out_sem.at[u])
        cp.start()
        outs.append(cp)
    for t in range(n_steps):
        for d in range(N_DEST):
            for k in range(4 * N_PART):
                copy_of(t, d, k).wait_send()
    for cp in outs:
        cp.wait()


def solution(mesh):
    n_rows, n_cols = mesh.shape["row"], mesh.shape["col"]

    def device_fn(w_one, w_two, inputs, targets):
        layers, width, hidden = w_one.shape[2:]
        steps, batch, _ = inputs.shape[2:]
        n_piece = 2 * layers * N_PART
        part = hidden // N_PART
        anywhere = pl.BlockSpec(memory_space=pl.ANY)
        o1, o2 = pl.pallas_call(
            functools.partial(kernel, n_rows, n_cols),
            out_shape=(jax.ShapeDtypeStruct((layers, width, hidden), F32), jax.ShapeDtypeStruct((layers, hidden, width), F32)),
            in_specs=[anywhere] * 4,
            out_specs=(anywhere, anywhere),
            scratch_shapes=[
                pltpu.VMEM((steps, batch, width), BF16),
                pltpu.VMEM((steps, batch, width), BF16),
                pltpu.VMEM((layers, hidden, width), F32),
                pltpu.VMEM((2 * layers, width, hidden), F32),
                pltpu.VMEM((2 * layers, width, hidden), BF16),
                pltpu.VMEM((layers, batch, hidden), BF16),
                pltpu.VMEM((layers, batch, hidden), F32),
                pltpu.VMEM((layers, batch, width), BF16),
                pltpu.VMEM((layers, width, batch), BF16),
                pltpu.VMEM((batch, width), F32),
                pltpu.VMEM((batch, width), BF16),
                pltpu.VMEM((batch, width), F32),
                pltpu.VMEM((batch, width), BF16),
                pltpu.VMEM((width, batch), BF16),
                pltpu.VMEM((width, hidden), F32),
                pltpu.VMEM((width, hidden), F32),
                pltpu.VMEM((steps, n_piece, width, part), BF16),
                pltpu.VMEM((steps, N_DEST, n_piece, width, part), BF16),
                pltpu.SemaphoreType.DMA((5 + 2 * steps,)),
                pltpu.SemaphoreType.DMA((2 * layers,)),
                pltpu.SemaphoreType.DMA((steps, N_DEST, n_piece)),
                pltpu.SemaphoreType.DMA((steps, N_DEST, n_piece)),
            ],
            compiler_params=pltpu.CompilerParams(collective_id=0, has_side_effects=True, vmem_limit_bytes=60 * 1024 * 1024),
        )(w_one[0, 0], w_two[0, 0], inputs[0, 0], targets[0, 0])
        return o1[None, None], o2[None, None]

    grid_spec = P("row", "col")
    return jax.shard_map(device_fn, mesh=mesh, in_specs=(grid_spec,) * 4, out_specs=(grid_spec, grid_spec), check_vma=False)
```

profile of v0, /device:TPU:0, one launch (start us, length us, event | category | flops | bytes accessed | tf_op | source)
XLA Modules:
  0.0 87.0 jit_solution(291175430818336392)
XLA Ops:
  0.6 82.6 %shard_map.59 = (f32[2,128,512]{2,1,0:T(8,128)}, f32[2,512,128]{2,1,0:T(8,128)}) custom-call(f32[2,128,512]{2,1,0:T(8,128)} %bitcast.10, f32[2,512,128]{2,1,0:T(8,128)} %bitcast.11, bf16[3,2048,128]{2,1,0:T(8,128)(2,1)} %bitcast.6, bf16[3,2048,128]{2,1,0:T(8,128)(2,1)} %bitcast.7), custom_call_target="tpu_custom_call" | custom-call | tf_op jit(solution)/shard_map/pallas_call | solution.py:247
  83.3 1.9 %copy.8 = f32[1,1,2,128,512]{4,3,2,1,0:T(8,128)} copy(f32[1,1,2,128,512]{4,3,2,1,0:T(8,128)} %bitcast.9) | data formatting | bytes 1048576
  85.1 1.9 %copy.9 = f32[1,1,2,512,128]{4,3,2,1,0:T(8,128)} copy(f32[1,1,2,512,128]{4,3,2,1,0:T(8,128)} %bitcast.8) | data formatting | bytes 1048576
where the time goes:
time: 87.2 us; the launch traced here: 87 us
  Pallas kernels  82.6 us (95%)
  local copies, waits for them, and re-layouts  3.74 us (4%)
    pallas_call x1, Pallas kernels, device_fn(): pl.pallas_call(functools.partial(kernel, n_rows, n_cols), out_shape=(jax....  82.6 us
    unnamed x2, local copies, waits for them, and re-layouts  3.74 us

commit v1 on v0

--- a/solution.py
+++ b/solution.py
@@ -36,7 +36,7 @@
 
 
 def kernel(n_rows, n_cols, w1_hbm, w2_hbm, x_hbm, t_hbm, o1_hbm, o2_hbm,
-           xs, ts, w2_in, master, wlo, act, slope, n_lo, n_tr, inv_b, hid, err, err_lo, err_tr, grad_a, grad_b,
+           xs, ts, w2_in, master, wlo, act, slope, n_lo, n_tr, inv_b, hid, err, err_lo, err_tr, dz,
            send, recv, in_sem, out_sem, send_sem, recv_sem):
     n_steps, batch, width = xs.shape
     hidden = act.shape[2]
@@ -63,34 +63,27 @@
     for dest in dests:
         pl.semaphore_signal(barrier, inc=1, device_id=dest, device_id_type=MESH)
 
-    def over_rows(size, body, unroll=1):
-        def step(i, carry):
-            body(pl.ds(pl.multiple_of(i * size, size), size))
-            return carry
-        lax.fori_loop(0, batch // size, step, 0, unroll=unroll)
+    def blocks(size):
+        return [slice(i, i + size) for i in range(0, batch, size)]
 
     def norm_of(x):
         return lax.rsqrt(jnp.mean(x * x, axis=-1, keepdims=True) + NORM_EPS)
 
     def prepare(t):
-        def body(rows):
+        for rows in blocks(256):
             x = xs[t, rows, :].astype(F32)
             n = (x * norm_of(x)).astype(BF16)
             n_lo[0, rows, :] = n
             n_tr[0, :, rows] = n.T
-        over_rows(512, body)
-
-    def hidden_phase(l, cols, sub=128):
-        def body(rows):
-            for s in range(rows.size // sub):
-                r = pl.ds(rows.start + s * sub, sub)
-                a, d = gelu_and_slope(dot(n_lo[l, r, :], wlo[2 * l, :, cols]))
-                act[l, r, cols] = a.astype(BF16)
-                slope[l, r, cols] = d
-        over_rows(512, body)
+
+    def hidden_phase(l, cols):
+        for rows in blocks(128):
+            a, d = gelu_and_slope(dot(n_lo[l, rows, :], wlo[2 * l, :, cols]))
+            act[l, rows, cols] = a.astype(BF16)
+            slope[l, rows, cols] = d
 
     def out0_phase(t):
-        def body(rows):
+        for rows in blocks(256):
             o = dot_rhs_t(act[0, rows, :], wlo[1])
             h = (xs[t, rows, :].astype(F32) + o).astype(BF16)
             hid[rows, :] = h
@@ -100,12 +93,10 @@
             inv_b[rows, :] = jnp.broadcast_to(inv, x.shape)
             n_lo[1, rows, :] = n
             n_tr[1, :, rows] = n.T
-        over_rows(512, body)
 
     def out1_phase(t):
         loss_scale = 2.0 / (batch * width)
-
-        def body(rows):
+        for rows in blocks(256):
             o = dot_rhs_t(act[1, rows, :], wlo[3])
             h = (hid[rows, :].astype(F32) + o).astype(BF16)
             e = loss_scale * (h.astype(F32) - ts[t, rows, :].astype(F32))
@@ -113,7 +104,21 @@
             err[rows, :] = e
             err_lo[rows, :] = lo
             err_tr[:, rows] = lo.T
-        over_rows(512, body)
+
+    def d_pre_phase(l):
+        for rows in blocks(512):
+            d_act = dot(err_lo[rows, :], wlo[2 * l + 1])
+            dz[rows, :] = (d_act * slope[l, rows, :]).astype(BF16)
+
+    def d_hidden_phase():
+        for rows in blocks(512):
+            m = dot_rhs_t(dz[rows, :], wlo[2])
+            inv = inv_b[rows, :]
+            n = hid[rows, :].astype(F32) * inv
+            e = err[rows, :] + inv * (m - n * jnp.mean(m * n, axis=-1, keepdims=True))
+            lo = e.astype(BF16)
+            err_lo[rows, :] = lo
+            err_tr[:, rows] = lo.T
 
     def update(t, u, grad):
         q = master[u] - LEARN_RATE * grad
@@ -144,32 +149,6 @@
         if t < n_steps - 1:
             wlo[u, :, cols] = p.astype(BF16)
 
-    def back1_phase():
-        grad_a[...] = jnp.zeros_like(grad_a)
-        grad_b[...] = jnp.zeros_like(grad_b)
-
-        def body(rows):
-            d_act = dot(err_lo[rows, :], wlo[3])
-            dz = (d_act * slope[1, rows, :]).astype(BF16)
-            grad_a[...] += dot(n_tr[1, :, rows], dz)
-            m = dot_rhs_t(dz, wlo[2])
-            inv = inv_b[rows, :]
-            n = hid[rows, :].astype(F32) * inv
-            e = err[rows, :] + inv * (m - n * jnp.mean(m * n, axis=-1, keepdims=True))
-            lo = e.astype(BF16)
-            err_lo[rows, :] = lo
-            grad_b[...] += dot(lo.T, act[0, rows, :])
-        over_rows(512, body)
-
-    def back0_phase():
-        grad_a[...] = jnp.zeros_like(grad_a)
-
-        def body(rows):
-            d_act = dot(err_lo[rows, :], wlo[1])
-            dz = (d_act * slope[0, rows, :]).astype(BF16)
-            grad_a[...] += dot(n_tr[0, :, rows], dz)
-        over_rows(512, body)
-
     halves = [slice(h * part, (h + 1) * part) for h in range(N_PART)]
     cp_x[0].wait()
     prepare(0)
@@ -203,20 +182,23 @@
         update(t, 3, dot(err_tr[...], act[1]))
         if t == 0:
             pl.semaphore_wait(barrier, N_DEST)
-        push(t, 6, 7)
-        back1_phase()
-        update(t, 2, grad_a[...])
-        update(t, 1, grad_b[...])
-        back0_phase()
-        update(t, 0, grad_a[...])
-        push(t, 0, 1, 2, 3, 4, 5)
+        push(t, 6)
+        d_pre_phase(1)
+        update(t, 2, dot(n_tr[1], dz[...]))
+        push(t, 4)
+        d_hidden_phase()
+        d_pre_phase(0)
+        update(t, 0, dot(n_tr[0], dz[...]))
+        push(t, 0, 1)
+        update(t, 1, dot(err_tr[...], act[0]))
+        push(t, 2, 3, 5, 7)
         if t < n_steps - 1:
             cp_x[t + 1].wait()
             prepare(t + 1)
 
     last = n_steps - 1
     outs = []
-    for u in (3, 0, 1, 2):
+    for u in (0, 1, 2, 3):
         l = u // 2
         for h in range(N_PART):
             combine(last, u * N_PART + h)
@@ -264,8 +246,7 @@
                 pltpu.VMEM((batch, width), F32),
                 pltpu.VMEM((batch, width), BF16),
                 pltpu.VMEM((width, batch), BF16),
-                pltpu.VMEM((width, hidden), F32),
-                pltpu.VMEM((width, hidden), F32),
+                pltpu.VMEM((batch, hidden), BF16),
                 pltpu.VMEM((steps, n_piece, width, part), BF16),
                 pltpu.VMEM((steps, N_DEST, n_piece, width, part), BF16),
                 pltpu.SemaphoreType.DMA((5 + 2 * steps,)),

time: 87.2 us -> 70.7 us (0.81)
  Pallas kernels: 82.6 us -> 66.1 us
    pallas_call x1, Pallas kernels: 82.6 us -> 66.1 us  [device_fn(): pl.pallas_call(functools.partial(kernel, n_rows, n_cols), out_shape=(jax....]
where the time goes in v1:
time: 70.7 us; the launch traced here: 70.5 us
  Pallas kernels  66.1 us (93%)
  local copies, waits for them, and re-layouts  3.74 us (5%)
    pallas_call x1, Pallas kernels, device_fn(): pl.pallas_call(functools.partial(kernel, n_rows, n_cols), out_shape=(jax....  66.1 us
    unnamed x2, local copies, waits for them, and re-layouts  3.74 us

profile of v1, /device:TPU:0, one launch (start us, length us, event | category | flops | bytes accessed | tf_op | source)
XLA Modules:
  0.0 70.5 jit_solution(1929778570305583057)
XLA Ops:
  0.6 66.1 %shard_map.59 = (f32[2,128,512]{2,1,0:T(8,128)}, f32[2,512,128]{2,1,0:T(8,128)}) custom-call(f32[2,128,512]{2,1,0:T(8,128)} %bitcast.10, f32[2,512,128]{2,1,0:T(8,128)} %bitcast.11, bf16[3,2048,128]{2,1,0:T(8,128)(2,1)} %bitcast.6, bf16[3,2048,128]{2,1,0:T(8,128)(2,1)} %bitcast.7), custom_call_target="tpu_custom_call" | custom-call | tf_op jit(solution)/shard_map/pallas_call | solution.py:229
  66.7 1.9 %copy.8 = f32[1,1,2,128,512]{4,3,2,1,0:T(8,128)} copy(f32[1,1,2,128,512]{4,3,2,1,0:T(8,128)} %bitcast.9) | data formatting | bytes 1048576
  68.6 1.9 %copy.9 = f32[1,1,2,512,128]{4,3,2,1,0:T(8,128)} copy(f32[1,1,2,512,128]{4,3,2,1,0:T(8,128)} %bitcast.8) | data formatting | bytes 1048576

commit v2 on v1

v2 whole, which is shorter than its diff:
```python
import functools

import jax
import jax.numpy as jnp
from jax import lax
from jax.experimental import pallas as pl
from jax.experimental.pallas import tpu as pltpu
from jax.sharding import PartitionSpec as P

LEARN_RATE = 1.5
NORM_EPS = 1e-6
GELU_C = 0.7978845608028654
GELU_K = 0.044715
MESH = pl.DeviceIdType.MESH
F32 = jnp.float32
BF16 = jnp.bfloat16
N_DEST = 3
N_PART = 4


def dot(lhs, rhs):
    return lax.dot_general(lhs, rhs, (((1,), (0,)), ((), ())), preferred_element_type=F32)


def dot_rhs_t(lhs, rhs):
    return lax.dot_general(lhs, rhs, (((1,), (1,)), ((), ())), preferred_element_type=F32)


def gelu_and_slope(z):
    cubic = (GELU_C * GELU_K * z) * z
    th = jnp.tanh(z * (GELU_C + cubic))
    half = 0.5 + 0.5 * th
    act = z * half
    slope = half + act * (1.0 - th) * (GELU_C + 3.0 * cubic)
    return act, slope


def gelu_value(z):
    return z * (0.5 + 0.5 * jnp.tanh(z * (GELU_C + (GELU_C * GELU_K * z) * z)))


def kernel(n_rows, n_cols, w1_hbm, w2_hbm, x_hbm, t_hbm, o1, o2,
           xs, ts, w2_in, master, wlo, act, slope, n_lo, n_tr, inv_b, hid, err, err_lo, err_tr, dz,
           send, recv, in_sem, send_sem, recv_sem):
    n_steps, batch, width = xs.shape
    hidden = act.shape[2]
    part, half = hidden // N_PART, hidden // 2
    halves = [slice(0, half), slice(half, hidden)]
    row, col = lax.axis_index("row"), lax.axis_index("col")
    nxt, prv = lax.rem(col + 1, n_cols), lax.rem(col + n_cols - 1, n_cols)
    dests = ((row, nxt), (row, prv), (lax.rem(row + 1, n_rows), col))

    def start(src, dst, idx):
        cp = pltpu.make_async_copy(src, dst, in_sem.at[idx])
        cp.start()
        return cp

    cp_x, cp_t = [None] * n_steps, [None] * n_steps
    cp_x[0] = start(x_hbm.at[0], xs.at[0], 0)
    cp_w1 = [start(w1_hbm.at[l], master.at[2 * l], 1 + l) for l in range(2)]
    cp_w2 = [start(w2_hbm.at[l], w2_in.at[l], 3 + l) for l in range(2)]
    for t in range(n_steps):
        if t:
            cp_x[t] = start(x_hbm.at[t], xs.at[t], 4 + 2 * t)
        cp_t[t] = start(t_hbm.at[t], ts.at[t], 5 + 2 * t)

    barrier = pltpu.get_barrier_semaphore()
    for dest in dests:
        pl.semaphore_signal(barrier, inc=1, device_id=dest, device_id_type=MESH)

    def blocks(size):
        return [slice(i, i + size) for i in range(0, batch, size)]

    def norm_of(x):
        return lax.rsqrt(jnp.mean(x * x, axis=-1, keepdims=True) + NORM_EPS)

    def prepare(t):
        for rows in blocks(256):
            x = xs[t, rows, :].astype(F32)
            n_lo[0, rows, :] = (x * norm_of(x)).astype(BF16)

    def prepare_tr():
        for rows in blocks(256):
            n_tr[0, :, rows] = n_lo[0, rows, :].T

    def hidden_phase(l, cols, late):
        for rows in blocks(128):
            z = dot(n_lo[l, rows, :], wlo[2 * l, :, cols])
            if late:
                a, d = gelu_value(z), z
            else:
                a, d = gelu_and_slope(z)
            act[l, rows, cols] = a.astype(BF16)
            slope[l, rows, cols] = d

    def first_half(l, partial):
        for rows in blocks(256):
            partial[rows, :] = dot_rhs_t(act[l, rows, halves[0]], wlo[2 * l + 1, :, halves[0]])

    def product(l, rows, partial):
        if partial is None:
            return dot_rhs_t(act[l, rows, :], wlo[2 * l + 1])
        return partial[rows, :] + dot_rhs_t(act[l, rows, halves[1]], wlo[2 * l + 1, :, halves[1]])

    def out0_phase(t, partial):
        for rows in blocks(256):
            h = (xs[t, rows, :].astype(F32) + product(0, rows, partial)).astype(BF16)
            hid[rows, :] = h
            x = h.astype(F32)
            inv = norm_of(x)
            n = (x * inv).astype(BF16)
            inv_b[rows, :] = jnp.broadcast_to(inv, x.shape)
            n_lo[1, rows, :] = n
            n_tr[1, :, rows] = n.T

    def out1_phase(t, partial):
        loss_scale = 2.0 / (batch * width)
        for rows in blocks(256):
            h = (hid[rows, :].astype(F32) + product(1, rows, partial)).astype(BF16)
            e = loss_scale * (h.astype(F32) - ts[t, rows, :].astype(F32))
            lo = e.astype(BF16)
            err[rows, :] = e
            err_lo[rows, :] = lo
            err_tr[:, rows] = lo.T

    def d_pre_phase(l, late):
        for rows in blocks(512):
            d_act = dot(err_lo[rows, :], wlo[2 * l + 1])
            d = slope[l, rows, :]
            if late:
                d = gelu_and_slope(d)[1]
            dz[rows, :] = (d_act * d).astype(BF16)

    def d_hidden_phase():
        for rows in blocks(512):
            m = dot_rhs_t(dz[rows, :], wlo[2])
            inv = inv_b[rows, :]
            n = hid[rows, :].astype(F32) * inv
            e = err[rows, :] + inv * (m - n * jnp.mean(m * n, axis=-1, keepdims=True))
            lo = e.astype(BF16)
            err_lo[rows, :] = lo
            err_tr[:, rows] = lo.T

    def update(t, u, left, right, cols):
        q = master[u, :, cols] - LEARN_RATE * dot(left[...], right[:, cols])
        master[u, :, cols] = q
        lo = q.astype(BF16)
        for j in range(0, q.shape[1], part):
            send[t, u * N_PART + (cols.start + j) // part] = lo[:, j:j + part]

    def copy_of(t, d, k):
        return pltpu.make_async_remote_copy(
            src_ref=send.at[t, k], dst_ref=recv.at[t, d, k], send_sem=send_sem.at[t, d, k],
            recv_sem=recv_sem.at[t, d, k], device_id=dests[d], device_id_type=MESH)

    def push(t, u, *hs):
        for h in hs:
            for d in range(N_DEST):
                copy_of(t, d, u * N_PART + h).start()

    def combine(t, u, *hs):
        for h in hs:
            k = u * N_PART + h
            for d in range(N_DEST):
                copy_of(t, d, k).wait_recv()
            cols = slice(h * part, (h + 1) * part)
            other = recv[t, 2, k].astype(F32)
            total = master[u, :, cols] + recv[t, 0, k].astype(F32) + recv[t, 1, k].astype(F32) + other + other
            p = total / 5.0
            if t < n_steps - 1:
                master[u, :, cols] = p
                wlo[u, :, cols] = p.astype(BF16)
            elif u % 2:
                o2[u // 2, cols, :] = p.T
            else:
                o1[u // 2, :, cols] = p

    everything = slice(0, hidden)
    cp_x[0].wait()
    prepare(0)
    for l in range(2):
        cp_w1[l].wait()
        wlo[2 * l] = master[2 * l].astype(BF16)
    for l in range(2):
        cp_w2[l].wait()
        w = w2_in[l].T
        master[2 * l + 1] = w
        wlo[2 * l + 1] = w.astype(BF16)

    for t in range(n_steps):
        first = t == 0
        if first:
            hidden_phase(0, everything, True)
            out0_phase(t, None)
            hidden_phase(1, everything, False)
            cp_t[t].wait()
            out1_phase(t, None)
        else:
            combine(t - 1, 0, 0, 1)
            hidden_phase(0, halves[0], False)
            combine(t - 1, 0, 2, 3)
            hidden_phase(0, halves[1], False)
            combine(t - 1, 1, 0, 1)
            first_half(0, inv_b)
            combine(t - 1, 1, 2, 3)
            out0_phase(t, inv_b)
            combine(t - 1, 2, 0, 1)
            hidden_phase(1, halves[0], False)
            combine(t - 1, 3, 0, 1)
            first_half(1, err)
            combine(t - 1, 2, 2, 3)
            hidden_phase(1, halves[1], False)
            cp_t[t].wait()
            combine(t - 1, 3, 2, 3)
            out1_phase(t, err)
        update(t, 3, err_tr, act.at[1], halves[0])
        if first:
            pl.semaphore_wait(barrier, N_DEST)
        push(t, 3, 0, 1)
        update(t, 3, err_tr, act.at[1], halves[1])
        d_pre_phase(1, False)
        update(t, 2, n_tr.at[1], dz, everything)
        push(t, 2, 0, 1, 2)
        if first:
            prepare_tr()
        d_hidden_phase()
        d_pre_phase(0, first)
        update(t, 0, n_tr.at[0], dz, everything)
        push(t, 0, 0, 1, 2, 3)
        update(t, 1, err_tr, act.at[0], everything)
        push(t, 1, 0, 1, 2, 3)
        push(t, 2, 3)
        push(t, 3, 2, 3)
        if t < n_steps - 1:
            cp_x[t + 1].wait()
            prepare(t + 1)
            prepare_tr()

    last = n_steps - 1
    combine(last, 3, 0, 1)
    combine(last, 2, 0, 1, 2)
    combine(last, 0, 0, 1, 2, 3)
    combine(last, 1, 0, 1, 2, 3)
    combine(last, 2, 3)
    combine(last, 3, 2, 3)
    for t in range(n_steps):
        for d in range(N_DEST):
            for k in range(4 * N_PART):
                copy_of(t, d, k).wait_send()


def solution(mesh):
    n_rows, n_cols = mesh.shape["row"], mesh.shape["col"]

    def device_fn(w_one, w_two, inputs, targets):
        layers, width, hidden = w_one.shape[2:]
        steps, batch, _ = inputs.shape[2:]
        n_piece = 2 * layers * N_PART
        part = hidden // N_PART
        in_spec = pl.BlockSpec(memory_space=pltpu.HBM)
        out_spec = pl.BlockSpec(memory_space=pltpu.VMEM)
        o1, o2 = pl.pallas_call(
            functools.partial(kernel, n_rows, n_cols),
            out_shape=(jax.ShapeDtypeStruct((layers, width, hidden), F32), jax.ShapeDtypeStruct((layers, hidden, width), F32)),
            in_specs=[in_spec] * 4,
            out_specs=(out_spec, out_spec),
            scratch_shapes=[
                pltpu.VMEM((steps, batch, width), BF16),
                pltpu.VMEM((steps, batch, width), BF16),
                pltpu.VMEM((layers, hidden, width), F32),
                pltpu.VMEM((2 * layers, width, hidden), F32),
                pltpu.VMEM((2 * layers, width, hidden), BF16),
                pltpu.VMEM((layers, batch, hidden), BF16),
                pltpu.VMEM((layers, batch, hidden), F32),
                pltpu.VMEM((layers, batch, width), BF16),
                pltpu.VMEM((layers, width, batch), BF16),
                pltpu.VMEM((batch, width), F32),
                pltpu.VMEM((batch, width), BF16),
                pltpu.VMEM((batch, width), F32),
                pltpu.VMEM((batch, width), BF16),
                pltpu.VMEM((width, batch), BF16),
                pltpu.VMEM((batch, hidden), BF16),
                pltpu.VMEM((steps, n_piece, width, part), BF16),
                pltpu.VMEM((steps, N_DEST, n_piece, width, part), BF16),
                pltpu.SemaphoreType.DMA((5 + 2 * steps,)),
                pltpu.SemaphoreType.DMA((steps, N_DEST, n_piece)),
                pltpu.SemaphoreType.DMA((steps, N_DEST, n_piece)),
            ],
            compiler_params=pltpu.CompilerParams(collective_id=0, has_side_effects=True, vmem_limit_bytes=48 * 1024 * 1024),
        )(*[pltpu.with_memory_space_constraint(v[0, 0], pltpu.HBM) for v in (w_one, w_two, inputs, targets)])
        return o1[None, None], o2[None, None]

    grid_spec = P("row", "col")
    return jax.shard_map(device_fn, mesh=mesh, in_specs=(grid_spec,) * 4, out_specs=(grid_spec, grid_spec), check_vma=False)
```

time: 70.7 us -> 70.4 us (level)
  local copies, waits for them, and re-layouts: 3.74 us -> 1.59 us
  Pallas kernels: 66.1 us -> 68.1 us
    unnamed x2, local copies, waits for them, and re-layouts: 3.74 us -> 1.59 us
    pallas_call x1, Pallas kernels: 66.1 us -> 68.1 us  [device_fn(): pl.pallas_call(functools.partial(kernel, n_rows, n_cols), out_shape=(jax....]
where the time goes in v2:
time: 70.4 us; the launch traced here: 70.3 us
  Pallas kernels  68.1 us (97%)
  local copies, waits for them, and re-layouts  1.59 us (2%)
    pallas_call x1, Pallas kernels, device_fn(): pl.pallas_call(functools.partial(kernel, n_rows, n_cols), out_shape=(jax....  68.1 us
    unnamed x2, local copies, waits for them, and re-layouts  1.59 us

profile of v2, /device:TPU:0, one launch (start us, length us, event | category | flops | bytes accessed | tf_op | source)
XLA Modules:
  0.0 70.3 jit_solution(1260296431161368086)
XLA Ops:
  0.6 68.1 %shard_map.59 = (f32[2,128,512]{2,1,0:T(8,128)S(1)}, f32[2,512,128]{2,1,0:T(8,128)S(1)}) custom-call(f32[2,128,512]{2,1,0:T(8,128)} %bitcast.10, f32[2,512,128]{2,1,0:T(8,128)} %bitcast.11, bf16[3,2048,128]{2,1,0:T(8,128)(2,1)} %bitcast.8, bf16[3,2048,128]{2,1,0:T(8,128)(2,1)} %bitcast.9), custom_call_target="tpu_custom_call" | custom-call | tf_op jit(solution)/shard_map/pallas_call | solution.py:262
  68.7 0.8 %copy.8 = f32[1,1,2,128,512]{4,3,2,1,0:T(8,128)} copy(f32[1,1,2,128,512]{4,3,2,1,0:T(8,128)S(1)} %bitcast.7) | data formatting | bytes 1048576
  69.5 0.8 %copy.9 = f32[1,1,2,512,128]{4,3,2,1,0:T(8,128)} copy(f32[1,1,2,512,128]{4,3,2,1,0:T(8,128)S(1)} %bitcast.6) | data formatting | bytes 1048576

commit v3 on v2

--- a/solution.py
+++ b/solution.py
@@ -121,25 +121,25 @@
             lo = e.astype(BF16)
             err[rows, :] = e
             err_lo[rows, :] = lo
-            err_tr[:, rows] = lo.T
-
-    def d_pre_phase(l, late):
+            err_tr[1, :, rows] = lo.T
+
+    def d_pre_phase(l, cols, late):
         for rows in blocks(512):
-            d_act = dot(err_lo[rows, :], wlo[2 * l + 1])
-            d = slope[l, rows, :]
+            d_act = dot(err_lo[rows, :], wlo[2 * l + 1, :, cols])
+            d = slope[l, rows, cols]
             if late:
                 d = gelu_and_slope(d)[1]
-            dz[rows, :] = (d_act * d).astype(BF16)
+            dz[l, rows, cols] = (d_act * d).astype(BF16)
 
     def d_hidden_phase():
         for rows in blocks(512):
-            m = dot_rhs_t(dz[rows, :], wlo[2])
+            m = dot_rhs_t(dz[1, rows, :], wlo[2])
             inv = inv_b[rows, :]
             n = hid[rows, :].astype(F32) * inv
             e = err[rows, :] + inv * (m - n * jnp.mean(m * n, axis=-1, keepdims=True))
             lo = e.astype(BF16)
             err_lo[rows, :] = lo
-            err_tr[:, rows] = lo.T
+            err_tr[0, :, rows] = lo.T
 
     def update(t, u, left, right, cols):
         q = master[u, :, cols] - LEARN_RATE * dot(left[...], right[:, cols])
@@ -196,6 +196,8 @@
             cp_t[t].wait()
             out1_phase(t, None)
         else:
+            combine(t - 1, 3, 0, 1)
+            combine(t - 1, 2, 0, 1)
             combine(t - 1, 0, 0, 1)
             hidden_phase(0, halves[0], False)
             combine(t - 1, 0, 2, 3)
@@ -204,32 +206,33 @@
             first_half(0, inv_b)
             combine(t - 1, 1, 2, 3)
             out0_phase(t, inv_b)
-            combine(t - 1, 2, 0, 1)
             hidden_phase(1, halves[0], False)
-            combine(t - 1, 3, 0, 1)
-            first_half(1, err)
             combine(t - 1, 2, 2, 3)
             hidden_phase(1, halves[1], False)
             cp_t[t].wait()
             combine(t - 1, 3, 2, 3)
-            out1_phase(t, err)
-        update(t, 3, err_tr, act.at[1], halves[0])
+            out1_phase(t, None)
+        update(t, 3, err_tr.at[1], act.at[1], halves[0])
         if first:
             pl.semaphore_wait(barrier, N_DEST)
         push(t, 3, 0, 1)
-        update(t, 3, err_tr, act.at[1], halves[1])
-        d_pre_phase(1, False)
-        update(t, 2, n_tr.at[1], dz, everything)
-        push(t, 2, 0, 1, 2)
+        d_pre_phase(1, everything, False)
+        update(t, 2, n_tr.at[1], dz.at[1], halves[0])
+        push(t, 2, 0, 1)
+        d_hidden_phase()
         if first:
             prepare_tr()
-        d_hidden_phase()
-        d_pre_phase(0, first)
-        update(t, 0, n_tr.at[0], dz, everything)
-        push(t, 0, 0, 1, 2, 3)
-        update(t, 1, err_tr, act.at[0], everything)
+        d_pre_phase(0, halves[0], first)
+        update(t, 0, n_tr.at[0], dz.at[0], halves[0])
+        push(t, 0, 0, 1)
+        d_pre_phase(0, halves[1], first)
+        update(t, 0, n_tr.at[0], dz.at[0], halves[1])
+        push(t, 0, 2, 3)
+        update(t, 1, err_tr.at[0], act.at[0], everything)
         push(t, 1, 0, 1, 2, 3)
-        push(t, 2, 3)
+        update(t, 2, n_tr.at[1], dz.at[1], halves[1])
+        push(t, 2, 2, 3)
+        update(t, 3, err_tr.at[1], act.at[1], halves[1])
         push(t, 3, 2, 3)
         if t < n_steps - 1:
             cp_x[t + 1].wait()
@@ -238,10 +241,10 @@
 
     last = n_steps - 1
     combine(last, 3, 0, 1)
-    combine(last, 2, 0, 1, 2)
+    combine(last, 2, 0, 1)
     combine(last, 0, 0, 1, 2, 3)
     combine(last, 1, 0, 1, 2, 3)
-    combine(last, 2, 3)
+    combine(last, 2, 2, 3)
     combine(last, 3, 2, 3)
     for t in range(n_steps):
         for d in range(N_DEST):
@@ -278,8 +281,8 @@
                 pltpu.VMEM((batch, width), BF16),
                 pltpu.VMEM((batch, width), F32),
                 pltpu.VMEM((batch, width), BF16),
-                pltpu.VMEM((width, batch), BF16),
-                pltpu.VMEM((batch, hidden), BF16),
+                pltpu.VMEM((layers, width, batch), BF16),
+                pltpu.VMEM((layers, batch, hidden), BF16),
                 pltpu.VMEM((steps, n_piece, width, part), BF16),
                 pltpu.VMEM((steps, N_DEST, n_piece, width, part), BF16),
                 pltpu.SemaphoreType.DMA((5 + 2 * steps,)),

time: 70.4 us -> 67.2 us (0.955)
  Pallas kernels: 68.1 us -> 64.8 us
    pallas_call x1, Pallas kernels: 68.1 us -> 64.8 us  [device_fn(): pl.pallas_call(functools.partial(kernel, n_rows, n_cols), out_shape=(jax....]
where the time goes in v3:
time: 67.2 us; the launch traced here: 67.1 us
  Pallas kernels  64.8 us (96%)
  local copies, waits for them, and re-layouts  1.59 us (2%)
    pallas_call x1, Pallas kernels, device_fn(): pl.pallas_call(functools.partial(kernel, n_rows, n_cols), out_shape=(jax....  64.8 us
    unnamed x2, local copies, waits for them, and re-layouts  1.59 us

profile of v3, /device:TPU:0, one launch (start us, length us, event | category | flops | bytes accessed | tf_op | source)
XLA Modules:
  0.0 67.1 jit_solution(10947812132001972398)
XLA Ops:
  0.6 64.8 %shard_map.59 = (f32[2,128,512]{2,1,0:T(8,128)S(1)}, f32[2,512,128]{2,1,0:T(8,128)S(1)}) custom-call(f32[2,128,512]{2,1,0:T(8,128)} %bitcast.10, f32[2,512,128]{2,1,0:T(8,128)} %bitcast.11, bf16[3,2048,128]{2,1,0:T(8,128)(2,1)} %bitcast.8, bf16[3,2048,128]{2,1,0:T(8,128)(2,1)} %bitcast.9), custom_call_target="tpu_custom_call" | custom-call | tf_op jit(solution)/shard_map/pallas_call | solution.py:265
  65.5 0.8 %copy.8 = f32[1,1,2,128,512]{4,3,2,1,0:T(8,128)} copy(f32[1,1,2,128,512]{4,3,2,1,0:T(8,128)S(1)} %bitcast.7) | data formatting | bytes 1048576
  66.3 0.8 %copy.9 = f32[1,1,2,512,128]{4,3,2,1,0:T(8,128)} copy(f32[1,1,2,512,128]{4,3,2,1,0:T(8,128)S(1)} %bitcast.6) | data formatting | bytes 1048576

commit v4 on v3

--- a/solution.py
+++ b/solution.py
@@ -15,7 +15,8 @@
 F32 = jnp.float32
 BF16 = jnp.bfloat16
 N_DEST = 3
-N_PART = 4
+SKEW = 256
+N_PART = 2
 
 
 def dot(lhs, rhs):
@@ -55,14 +56,13 @@
         cp.start()
         return cp
 
-    cp_x, cp_t = [None] * n_steps, [None] * n_steps
-    cp_x[0] = start(x_hbm.at[0], xs.at[0], 0)
-    cp_w1 = [start(w1_hbm.at[l], master.at[2 * l], 1 + l) for l in range(2)]
-    cp_w2 = [start(w2_hbm.at[l], w2_in.at[l], 3 + l) for l in range(2)]
-    for t in range(n_steps):
-        if t:
-            cp_x[t] = start(x_hbm.at[t], xs.at[t], 4 + 2 * t)
-        cp_t[t] = start(t_hbm.at[t], ts.at[t], 5 + 2 * t)
+    cp_w1 = [None] * 2
+    cp_w1[0] = start(w1_hbm.at[0], master.at[0], 0)
+    cp_x0 = start(x_hbm.at[0], xs.at[0], 1)
+    cp_w2 = start(w2_hbm, w2_in, 2)
+    cp_w1[1] = start(w1_hbm.at[1], master.at[2], 3)
+    cp_t = start(t_hbm, ts, 4)
+    cp_x = start(x_hbm.at[pl.ds(1, n_steps - 1)], xs.at[pl.ds(1, n_steps - 1)], 5)
 
     barrier = pltpu.get_barrier_semaphore()
     for dest in dests:
@@ -74,24 +74,30 @@
     def norm_of(x):
         return lax.rsqrt(jnp.mean(x * x, axis=-1, keepdims=True) + NORM_EPS)
 
+    def prepare_rows(t, rows):
+        x = xs[t, rows, :].astype(F32)
+        n_lo[0, rows, :] = (x * norm_of(x)).astype(BF16)
+
     def prepare(t):
         for rows in blocks(256):
-            x = xs[t, rows, :].astype(F32)
-            n_lo[0, rows, :] = (x * norm_of(x)).astype(BF16)
+            prepare_rows(t, rows)
 
     def prepare_tr():
         for rows in blocks(256):
             n_tr[0, :, rows] = n_lo[0, rows, :].T
 
-    def hidden_phase(l, cols, late):
+    def hidden_rows(l, rows, cols, late):
+        z = dot(n_lo[l, rows, :], wlo[2 * l, :, cols])
+        if late:
+            a, d = gelu_value(z), z
+        else:
+            a, d = gelu_and_slope(z)
+        act[l, rows, cols] = a.astype(BF16)
+        slope[l, rows, cols] = d
+
+    def hidden_phase(l, cols):
         for rows in blocks(128):
-            z = dot(n_lo[l, rows, :], wlo[2 * l, :, cols])
-            if late:
-                a, d = gelu_value(z), z
-            else:
-                a, d = gelu_and_slope(z)
-            act[l, rows, cols] = a.astype(BF16)
-            slope[l, rows, cols] = d
+            hidden_rows(l, rows, cols, False)
 
     def first_half(l, partial):
         for rows in blocks(256):
@@ -102,26 +108,36 @@
             return dot_rhs_t(act[l, rows, :], wlo[2 * l + 1])
         return partial[rows, :] + dot_rhs_t(act[l, rows, halves[1]], wlo[2 * l + 1, :, halves[1]])
 
-    def out0_phase(t, partial):
-        for rows in blocks(256):
-            h = (xs[t, rows, :].astype(F32) + product(0, rows, partial)).astype(BF16)
-            hid[rows, :] = h
-            x = h.astype(F32)
-            inv = norm_of(x)
-            n = (x * inv).astype(BF16)
-            inv_b[rows, :] = jnp.broadcast_to(inv, x.shape)
-            n_lo[1, rows, :] = n
-            n_tr[1, :, rows] = n.T
-
-    def out1_phase(t, partial):
+    def out0_rows(t, rows, partial):
+        h = (xs[t, rows, :].astype(F32) + product(0, rows, partial)).astype(BF16)
+        hid[rows, :] = h
+        x = h.astype(F32)
+        inv = norm_of(x)
+        n = (x * inv).astype(BF16)
+        inv_b[rows, :] = jnp.broadcast_to(inv, x.shape)
+        n_lo[1, rows, :] = n
+        n_tr[1, :, rows] = n.T
+
+    def out1_rows(t, rows, partial):
         loss_scale = 2.0 / (batch * width)
-        for rows in blocks(256):
-            h = (hid[rows, :].astype(F32) + product(1, rows, partial)).astype(BF16)
-            e = loss_scale * (h.astype(F32) - ts[t, rows, :].astype(F32))
-            lo = e.astype(BF16)
-            err[rows, :] = e
-            err_lo[rows, :] = lo
-            err_tr[1, :, rows] = lo.T
+        h = (hid[rows, :].astype(F32) + product(1, rows, partial)).astype(BF16)
+        e = loss_scale * (h.astype(F32) - ts[t, rows, :].astype(F32))
+        lo = e.astype(BF16)
+        err[rows, :] = e
+        err_lo[rows, :] = lo
+        err_tr[1, :, rows] = lo.T
+
+    def skewed(size, *stages):
+        for i in range(batch // size + len(stages) - 1):
+            for j, stage in enumerate(stages):
+                if 0 <= i - j < batch // size:
+                    stage(slice((i - j) * size, (i - j + 1) * size))
+
+    def fine(stage):
+        def run(rows):
+            for lo in range(rows.start, rows.stop, 128):
+                stage(slice(lo, lo + 128))
+        return run
 
     def d_pre_phase(l, cols, late):
         for rows in blocks(512):
@@ -150,8 +166,12 @@
 
     def copy_of(t, d, k):
         return pltpu.make_async_remote_copy(
-            src_ref=send.at[t, k], dst_ref=recv.at[t, d, k], send_sem=send_sem.at[t, d, k],
-            recv_sem=recv_sem.at[t, d, k], device_id=dests[d], device_id_type=MESH)
+            src_ref=send.at[t, k], dst_ref=recv.at[t, k, d], send_sem=send_sem.at[0],
+            recv_sem=recv_sem.at[t, k], device_id=dests[d], device_id_type=MESH)
+
+    def all_of(ref, sem):
+        return pltpu.make_async_remote_copy(
+            src_ref=ref, dst_ref=ref, send_sem=sem, recv_sem=sem, device_id=dests[0], device_id_type=MESH)
 
     def push(t, u, *hs):
         for h in hs:
@@ -161,11 +181,10 @@
     def combine(t, u, *hs):
         for h in hs:
             k = u * N_PART + h
-            for d in range(N_DEST):
-                copy_of(t, d, k).wait_recv()
+            all_of(recv.at[t, k], recv_sem.at[t, k]).wait_recv()
             cols = slice(h * part, (h + 1) * part)
-            other = recv[t, 2, k].astype(F32)
-            total = master[u, :, cols] + recv[t, 0, k].astype(F32) + recv[t, 1, k].astype(F32) + other + other
+            other = recv[t, k, 2].astype(F32)
+            total = master[u, :, cols] + recv[t, k, 0].astype(F32) + recv[t, k, 1].astype(F32) + other + other
             p = total / 5.0
             if t < n_steps - 1:
                 master[u, :, cols] = p
@@ -176,80 +195,81 @@
                 o1[u // 2, :, cols] = p
 
     everything = slice(0, hidden)
-    cp_x[0].wait()
-    prepare(0)
-    for l in range(2):
-        cp_w1[l].wait()
-        wlo[2 * l] = master[2 * l].astype(BF16)
-    for l in range(2):
-        cp_w2[l].wait()
-        w = w2_in[l].T
-        master[2 * l + 1] = w
-        wlo[2 * l + 1] = w.astype(BF16)
+    cp_w1[0].wait()
+    wlo[0] = master[0].astype(BF16)
+    cp_x0.wait()
+    cp_w2.wait()
+    w = w2_in[0].T
+    master[1] = w
+    wlo[1] = w.astype(BF16)
 
     for t in range(n_steps):
         first = t == 0
         if first:
-            hidden_phase(0, everything, True)
-            out0_phase(t, None)
-            hidden_phase(1, everything, False)
-            cp_t[t].wait()
-            out1_phase(t, None)
+            skewed(
+                SKEW, functools.partial(prepare_rows, 0), fine(lambda rows: hidden_rows(0, rows, everything, True)),
+                lambda rows: out0_rows(0, rows, None))
+            cp_w1[1].wait()
+            wlo[2] = master[2].astype(BF16)
+            w = w2_in[1].T
+            master[3] = w
+            wlo[3] = w.astype(BF16)
+            cp_t.wait()
+            skewed(SKEW, fine(lambda rows: hidden_rows(1, rows, everything, False)), lambda rows: out1_rows(0, rows, None))
         else:
-            combine(t - 1, 3, 0, 1)
-            combine(t - 1, 2, 0, 1)
-            combine(t - 1, 0, 0, 1)
-            hidden_phase(0, halves[0], False)
-            combine(t - 1, 0, 2, 3)
-            hidden_phase(0, halves[1], False)
-            combine(t - 1, 1, 0, 1)
+            combine(t - 1, 3, 0)
+            combine(t - 1, 2, 0)
+            combine(t - 1, 0, 0)
+            hidden_phase(0, halves[0])
+            combine(t - 1, 0, 1)
+            hidden_phase(0, halves[1])
+            combine(t - 1, 1, 0)
             first_half(0, inv_b)
-            combine(t - 1, 1, 2, 3)
-            out0_phase(t, inv_b)
-            hidden_phase(1, halves[0], False)
-            combine(t - 1, 2, 2, 3)
-            hidden_phase(1, halves[1], False)
-            cp_t[t].wait()
-            combine(t - 1, 3, 2, 3)
-            out1_phase(t, None)
+            combine(t - 1, 1, 1)
+            for rows in blocks(256):
+                out0_rows(t, rows, inv_b)
+            hidden_phase(1, halves[0])
+            combine(t - 1, 2, 1)
+            hidden_phase(1, halves[1])
+            combine(t - 1, 3, 1)
+            for rows in blocks(256):
+                out1_rows(t, rows, None)
         update(t, 3, err_tr.at[1], act.at[1], halves[0])
         if first:
             pl.semaphore_wait(barrier, N_DEST)
-        push(t, 3, 0, 1)
+        push(t, 3, 0)
         d_pre_phase(1, everything, False)
         update(t, 2, n_tr.at[1], dz.at[1], halves[0])
-        push(t, 2, 0, 1)
+        push(t, 2, 0)
         d_hidden_phase()
         if first:
             prepare_tr()
         d_pre_phase(0, halves[0], first)
         update(t, 0, n_tr.at[0], dz.at[0], halves[0])
-        push(t, 0, 0, 1)
+        push(t, 0, 0)
         d_pre_phase(0, halves[1], first)
         update(t, 0, n_tr.at[0], dz.at[0], halves[1])
-        push(t, 0, 2, 3)
+        push(t, 0, 1)
         update(t, 1, err_tr.at[0], act.at[0], everything)
-        push(t, 1, 0, 1, 2, 3)
+        push(t, 1, 0, 1)
         update(t, 2, n_tr.at[1], dz.at[1], halves[1])
-        push(t, 2, 2, 3)
+        push(t, 2, 1)
         update(t, 3, err_tr.at[1], act.at[1], halves[1])
-        push(t, 3, 2, 3)
+        push(t, 3, 1)
+        if first:
+            cp_x.wait()
         if t < n_steps - 1:
-            cp_x[t + 1].wait()
             prepare(t + 1)
             prepare_tr()
 
     last = n_steps - 1
-    combine(last, 3, 0, 1)
-    combine(last, 2, 0, 1)
-    combine(last, 0, 0, 1, 2, 3)
-    combine(last, 1, 0, 1, 2, 3)
-    combine(last, 2, 2, 3)
-    combine(last, 3, 2, 3)
-    for t in range(n_steps):
-        for d in range(N_DEST):
-            for k in range(4 * N_PART):
-                copy_of(t, d, k).wait_send()
+    combine(last, 3, 0)
+    combine(last, 2, 0)
+    combine(last, 0, 0, 1)
+    combine(last, 1, 0, 1)
+    combine(last, 2, 1)
+    combine(last, 3, 1)
+    all_of(recv, send_sem.at[0]).wait_send()
 
 
 def solution(mesh):
@@ -284,10 +304,10 @@
                 pltpu.VMEM((layers, width, batch), BF16),
                 pltpu.VMEM((layers, batch, hidden), BF16),
                 pltpu.VMEM((steps, n_piece, width, part), BF16),
-                pltpu.VMEM((steps, N_DEST, n_piece, width, part), BF16),
-                pltpu.SemaphoreType.DMA((5 + 2 * steps,)),
-                pltpu.SemaphoreType.DMA((steps, N_DEST, n_piece)),
-                pltpu.SemaphoreType.DMA((steps, N_DEST, n_piece)),
+                pltpu.VMEM((steps, n_piece, N_DEST, width, part), BF16),
+                pltpu.SemaphoreType.DMA((6,)),
+                pltpu.SemaphoreType.DMA((1,)),
+                pltpu.SemaphoreType.DMA((steps, n_piece)),
             ],
             compiler_params=pltpu.CompilerParams(collective_id=0, has_side_effects=True, vmem_limit_bytes=48 * 1024 * 1024),
         )(*[pltpu.with_memory_space_constraint(v[0, 0], pltpu.HBM) for v in (w_one, w_two, inputs, targets)])

time: 67.2 us -> 64.1 us (0.954)
  Pallas kernels: 64.8 us -> 61.8 us
    pallas_call x1, Pallas kernels: 64.8 us -> 61.8 us  [device_fn(): pl.pallas_call(functools.partial(kernel, n_rows, n_cols), out_shape=(jax....]
where the time goes in v4:
time: 64.1 us; the launch traced here: 64 us
  Pallas kernels  61.8 us (96%)
  local copies, waits for them, and re-layouts  1.59 us (2%)
    pallas_call x1, Pallas kernels, device_fn(): pl.pallas_call(functools.partial(kernel, n_rows, n_cols), out_shape=(jax....  61.8 us
    unnamed x2, local copies, waits for them, and re-layouts  1.59 us

profile of v4, /device:TPU:0, one launch (start us, length us, event | category | flops | bytes accessed | tf_op | source)
XLA Modules:
  0.0 64.0 jit_solution(13770073692943485097)
XLA Ops:
  0.6 61.8 %shard_map.59 = (f32[2,128,512]{2,1,0:T(8,128)S(1)}, f32[2,512,128]{2,1,0:T(8,128)S(1)}) custom-call(f32[2,128,512]{2,1,0:T(8,128)} %bitcast.10, f32[2,512,128]{2,1,0:T(8,128)} %bitcast.11, bf16[3,2048,128]{2,1,0:T(8,128)(2,1)} %bitcast.8, bf16[3,2048,128]{2,1,0:T(8,128)(2,1)} %bitcast.9), custom_call_target="tpu_custom_call" | custom-call | tf_op jit(solution)/shard_map/pallas_call | solution.py:285
  62.4 0.8 %copy.8 = f32[1,1,2,128,512]{4,3,2,1,0:T(8,128)} copy(f32[1,1,2,128,512]{4,3,2,1,0:T(8,128)S(1)} %bitcast.7) | data formatting | bytes 1048576
  63.2 0.8 %copy.9 = f32[1,1,2,512,128]{4,3,2,1,0:T(8,128)} copy(f32[1,1,2,512,128]{4,3,2,1,0:T(8,128)S(1)} %bitcast.6) | data formatting | bytes 1048576

commit v5 on v4

--- a/solution.py
+++ b/solution.py
@@ -15,7 +15,7 @@
 F32 = jnp.float32
 BF16 = jnp.bfloat16
 N_DEST = 3
-SKEW = 256
+SKEW = 512
 N_PART = 2
 
 
@@ -252,10 +252,14 @@
         push(t, 0, 1)
         update(t, 1, err_tr.at[0], act.at[0], everything)
         push(t, 1, 0, 1)
-        update(t, 2, n_tr.at[1], dz.at[1], halves[1])
-        push(t, 2, 1)
+        if t < n_steps - 1:
+            update(t, 2, n_tr.at[1], dz.at[1], halves[1])
+            push(t, 2, 1)
         update(t, 3, err_tr.at[1], act.at[1], halves[1])
         push(t, 3, 1)
+        if t == n_steps - 1:
+            update(t, 2, n_tr.at[1], dz.at[1], halves[1])
+            push(t, 2, 1)
         if first:
             cp_x.wait()
         if t < n_steps - 1:
@@ -267,9 +271,17 @@
     combine(last, 2, 0)
     combine(last, 0, 0, 1)
     combine(last, 1, 0, 1)
+    combine(last, 3, 1)
     combine(last, 2, 1)
-    combine(last, 3, 1)
     all_of(recv, send_sem.at[0]).wait_send()
+
+
+def store(a, b, out_a, out_b, sem):
+    copies = [pltpu.make_async_copy(a, out_a, sem.at[0]), pltpu.make_async_copy(b, out_b, sem.at[1])]
+    for cp in copies:
+        cp.start()
+    for cp in copies:
+        cp.wait()
 
 
 def solution(mesh):
@@ -311,6 +323,14 @@
             ],
             compiler_params=pltpu.CompilerParams(collective_id=0, has_side_effects=True, vmem_limit_bytes=48 * 1024 * 1024),
         )(*[pltpu.with_memory_space_constraint(v[0, 0], pltpu.HBM) for v in (w_one, w_two, inputs, targets)])
+        o1, o2 = pl.pallas_call(
+            store,
+            out_shape=(jax.ShapeDtypeStruct(o1.shape, F32), jax.ShapeDtypeStruct(o2.shape, F32)),
+            in_specs=[pl.BlockSpec(memory_space=pl.ANY)] * 2,
+            out_specs=(pl.BlockSpec(memory_space=pl.ANY),) * 2,
+            scratch_shapes=[pltpu.SemaphoreType.DMA((2,))],
+            compiler_params=pltpu.CompilerParams(vmem_limit_bytes=1024 * 1024),
+        )(o1, o2)
         return o1[None, None], o2[None, None]
 
     grid_spec = P("row", "col")

time: 64.1 us -> 63.7 us (level)
  local copies, waits for them, and re-layouts: 1.59 us -> 0 us
  Pallas kernels: 61.8 us -> 62.8 us
    unnamed x2 -> x0, local copies, waits for them, and re-layouts: 1.59 us -> none
    pallas_call x0 -> x1, Pallas kernels: none -> 0.99 us  [device_fn(): pl.pallas_call(store, out_shape=(jax.ShapeDtypeStruct(o1.shape, F32), jax...]
where the time goes in v5:
time: 63.7 us; the launch traced here: 63.6 us
  Pallas kernels  62.8 us (99%)
  between operations  0.82 us (1%)
    pallas_call x1, Pallas kernels, device_fn(): pl.pallas_call(functools.partial(kernel, n_rows, n_cols), out_shape=(jax....  61.8 us

profile of v5, /device:TPU:0, one launch (start us, length us, event | category | flops | bytes accessed | tf_op | source)
XLA Modules:
  0.0 63.6 jit_solution(6510060798597696426)
XLA Ops:
  0.6 61.8 %shard_map.59 = (f32[2,128,512]{2,1,0:T(8,128)S(1)}, f32[2,512,128]{2,1,0:T(8,128)S(1)}) custom-call(f32[2,128,512]{2,1,0:T(8,128)} %bitcast.8, f32[2,512,128]{2,1,0:T(8,128)} %bitcast.9, bf16[3,2048,128]{2,1,0:T(8,128)(2,1)} %bitcast.6, bf16[3,2048,128]{2,1,0:T(8,128)(2,1)} %bitcast.7), custom_call_target="tpu_custom_call" | custom-call | tf_op jit(solution)/shard_map/pallas_call | solution.py:297
  62.4 1.0 %shard_map.60 = (f32[2,128,512]{2,1,0:T(8,128)}, f32[2,512,128]{2,1,0:T(8,128)}) custom-call(f32[2,128,512]{2,1,0:T(8,128)S(1)} %get-tuple-element.6.a, f32[2,512,128]{2,1,0:T(8,128)S(1)} %get-tuple-element.7.b), custom_call_target="tpu_custom_call" | custom-call | tf_op jit(solution)/shard_map/pallas_call | solution.py:326

commit v6 on v5

--- a/solution.py
+++ b/solution.py
@@ -167,7 +167,7 @@
     def copy_of(t, d, k):
         return pltpu.make_async_remote_copy(
             src_ref=send.at[t, k], dst_ref=recv.at[t, k, d], send_sem=send_sem.at[0],
-            recv_sem=recv_sem.at[t, k], device_id=dests[d], device_id_type=MESH)
+            recv_sem=recv_sem.at[t % 2, k], device_id=dests[d], device_id_type=MESH)
 
     def all_of(ref, sem):
         return pltpu.make_async_remote_copy(
@@ -181,7 +181,7 @@
     def combine(t, u, *hs):
         for h in hs:
             k = u * N_PART + h
-            all_of(recv.at[t, k], recv_sem.at[t, k]).wait_recv()
+            all_of(recv.at[t, k], recv_sem.at[t % 2, k]).wait_recv()
             cols = slice(h * part, (h + 1) * part)
             other = recv[t, k, 2].astype(F32)
             total = master[u, :, cols] + recv[t, k, 0].astype(F32) + recv[t, k, 1].astype(F32) + other + other
@@ -231,9 +231,10 @@
             hidden_phase(1, halves[0])
             combine(t - 1, 2, 1)
             hidden_phase(1, halves[1])
+            first_half(1, err)
             combine(t - 1, 3, 1)
             for rows in blocks(256):
-                out1_rows(t, rows, None)
+                out1_rows(t, rows, err)
         update(t, 3, err_tr.at[1], act.at[1], halves[0])
         if first:
             pl.semaphore_wait(barrier, N_DEST)
@@ -319,7 +320,7 @@
                 pltpu.VMEM((steps, n_piece, N_DEST, width, part), BF16),
                 pltpu.SemaphoreType.DMA((6,)),
                 pltpu.SemaphoreType.DMA((1,)),
-                pltpu.SemaphoreType.DMA((steps, n_piece)),
+                pltpu.SemaphoreType.DMA((2, n_piece)),
             ],
             compiler_params=pltpu.CompilerParams(collective_id=0, has_side_effects=True, vmem_limit_bytes=48 * 1024 * 1024),
         )(*[pltpu.with_memory_space_constraint(v[0, 0], pltpu.HBM) for v in (w_one, w_two, inputs, targets)])

time: 63.7 us -> 63.6 us (level)
  no operation moved by 1% of the time
where the time goes in v6:
time: 63.6 us; the launch traced here: 63.5 us
  Pallas kernels  62.7 us (99%)
  between operations  0.82 us (1%)
    pallas_call x1, Pallas kernels, device_fn(): pl.pallas_call(functools.partial(kernel, n_rows, n_cols), out_shape=(jax....  61.7 us

profile of v6, /device:TPU:0, one launch (start us, length us, event | category | flops | bytes accessed | tf_op | source)
XLA Modules:
  0.0 63.5 jit_solution(7642427232861722042)
XLA Ops:
  0.6 61.7 %shard_map.59 = (f32[2,128,512]{2,1,0:T(8,128)S(1)}, f32[2,512,128]{2,1,0:T(8,128)S(1)}) custom-call(f32[2,128,512]{2,1,0:T(8,128)} %bitcast.8, f32[2,512,128]{2,1,0:T(8,128)} %bitcast.9, bf16[3,2048,128]{2,1,0:T(8,128)(2,1)} %bitcast.6, bf16[3,2048,128]{2,1,0:T(8,128)(2,1)} %bitcast.7), custom_call_target="tpu_custom_call" | custom-call | tf_op jit(solution)/shard_map/pallas_call | solution.py:298
  62.3 1.0 %shard_map.60 = (f32[2,128,512]{2,1,0:T(8,128)}, f32[2,512,128]{2,1,0:T(8,128)}) custom-call(f32[2,128,512]{2,1,0:T(8,128)S(1)} %get-tuple-element.6.a, f32[2,512,128]{2,1,0:T(8,128)S(1)} %get-tuple-element.7.b), custom_call_target="tpu_custom_call" | custom-call | tf_op jit(solution)/shard_map/pallas_call | solution.py:327
